TPU v7x, 32 devices: a whole 2x2x4 slice. The times are simulated.
32 devices in a mesh: rep: 4 (over y, core), row: 4 (over z), col: 2 (over x).
Axes of the slice: x: 2, y: 2, z: 4, core: 2. Of those that a mesh axis runs over, the one named last changes fastest.
Arguments:
- patches: bfloat16 [4096, 588], P(('rep', 'col')), may hold values from -20 to 20
- embed_weight: bfloat16 [588, 6144], P(None, 'row'), may hold values from -1 to 1
- embed_bias: float32 [6144], P('row'), may hold values from -3 to 3
- old_in: bfloat16 [64, 768, 1536], P(('row', 'col')), may hold values from -0.078125 to 0.078125
- old_out: bfloat16 [64, 1536, 768], P(('row', 'col')), may hold values from -0.0546875 to 0.0546875
- restore_id: int32 [1], replicated, may hold values from 0 to 47
- norm_gains: float32 [48, 6144], P(None, 'row'), may hold values from 0.1 to 1.9
- in_biases: float32 [48, 12288], P(None, 'col'), may hold values from -3 to 3
- out_biases: float32 [48, 6144], P(None, 'row'), may hold values from -3 to 3
- final_gain: float32 [6144], P('row'), may hold values from 0.1 to 1.9
- check_weight: bfloat16 [6144, 128], P('row'), may hold values from -0.078125 to 0.078125
Outputs:
- in_weight: bfloat16 [6144, 12288], P('row', 'col')
- out_weight: bfloat16 [12288, 6144], P('col', 'row')
- check_logits: float32 [4096, 128], P(('rep', 'col'))
All inputs are finite; a program needn't handle non-finite values.
Results may differ from a plain program's by a relative error of at most 0.0062.
Values may be sent and summed in bfloat16 or wider, within the bound.
A program may use at most 192 MiB of HBM per device.

v0:
```python
import jax
import jax.numpy as jnp
from jax import lax
from jax.sharding import PartitionSpec as P

EPSILON = 1e-06


def for_sending(shard):
    return jax.tree.map(lambda a: a.astype(jnp.bfloat16) if a.dtype == jnp.float32 else a, shard)


def partner(value, axis, bit):
    mask = 2**bit
    pairs = [(source, source ^ mask) for source in range(lax.axis_size(axis))]
    return lax.ppermute(value, axis, pairs)


def pick_rows(restore_id, param_table):
    selector = (
        jnp.arange(param_table.shape[0], dtype=jnp.int32)[None, :] == restore_id[:, None]
    ).astype(jnp.float32)
    return jnp.dot(selector, param_table, precision=lax.Precision.HIGHEST)[0]


def norm_rows(values, gain_row):
    feature_count = values.shape[1] * lax.axis_size("row")
    totals = lax.psum((jnp.sum(values, axis=1), jnp.sum(values * values, axis=1)), "row")
    average = totals[0][:, None] / feature_count
    spread = totals[1][:, None] / feature_count - average * average
    return ((values - average) * lax.rsqrt(spread + EPSILON) * gain_row).astype(jnp.bfloat16)


def move_halves(pieces, bit_total, device_index, exchange):
    for bit_number in range(bit_total):
        upper_side = device_index >> bit_number & 1 == 1
        outgoing = tuple(
            (jnp.where(upper_side, lower_part, upper_part) for lower_part, upper_part in pieces)
        )
        incoming = exchange(outgoing, bit_number)
        pieces = tuple(
            (
                (
                    jnp.where(upper_side, arrived, lower_part),
                    jnp.where(upper_side, upper_part, arrived),
                )
                for (lower_part, upper_part), arrived in zip(pieces, incoming)
            )
        )
    return pieces


def on_device(
    patches,
    embed_weight,
    embed_bias,
    old_in,
    old_out,
    restore_id,
    norm_gains,
    in_biases,
    out_biases,
    final_gain,
    check_weight,
):
    tiles_here, tile_rows, tile_cols = old_in.shape
    local_cols = tiles_here * tile_cols
    half_cols = local_cols // 2
    in_local = jnp.transpose(old_in, (1, 0, 2)).reshape(tile_rows, local_cols)
    out_local = old_out.reshape(local_cols, tile_rows)
    col_index = lax.axis_index("col")
    col_count = lax.axis_size("col")
    col_bits = col_count.bit_length() - 1
    pieces = (
        (in_local[:, :half_cols], in_local[:, half_cols:]),
        (out_local[:half_cols], out_local[half_cols:]),
    )
    pieces = move_halves(
        pieces,
        col_bits,
        col_index,
        lambda send_parts, bit_number: jax.tree.map(
            lambda part, own: part.astype(own.dtype),
            partner(for_sending(send_parts), "col", bit_number),
            send_parts,
        ),
    )
    in_pair, out_pair = pieces
    in_weight = jnp.concatenate(in_pair, axis=0)
    out_weight = jnp.concatenate(out_pair, axis=1)
    layer_gain = pick_rows(restore_id, norm_gains)
    in_bias = pick_rows(restore_id, in_biases)
    out_bias = pick_rows(restore_id, out_biases)
    embedded = jnp.dot(patches, embed_weight, preferred_element_type=jnp.float32) + embed_bias
    normed = norm_rows(embedded, layer_gain)
    partial_pre = jnp.dot(
        lax.all_gather(normed, "col", axis=0, tiled=True),
        in_weight,
        preferred_element_type=jnp.float32,
    )
    pre_share = lax.psum_scatter(partial_pre, "row", scatter_dimension=0, tiled=True) + in_bias
    hidden = jax.nn.gelu(pre_share, approximate=False).astype(jnp.bfloat16)
    partial_branch = jnp.dot(
        lax.all_gather(hidden, "row", axis=0, tiled=True),
        out_weight,
        preferred_element_type=jnp.float32,
    )
    updated = (
        embedded
        + lax.psum_scatter(partial_branch, "col", scatter_dimension=0, tiled=True)
        + out_bias
    )
    final_normed = norm_rows(updated, final_gain)
    check_logits = lax.psum(
        jnp.dot(final_normed, check_weight, preferred_element_type=jnp.float32), "row"
    )
    return (in_weight, out_weight, check_logits)


def solution(mesh):
    placed = (
        P(("rep", "col"), None),
        P(None, "row"),
        P("row"),
        P(("row", "col"), None, None),
        P(("row", "col"), None, None),
        P(),
        P(None, "row"),
        P(None, "col"),
        P(None, "row"),
        P("row"),
        P("row", None),
    )
    return jax.shard_map(
        on_device,
        mesh=mesh,
        in_specs=placed,
        out_specs=(P("row", "col"), P("col", "row"), P(("rep", "col"), None)),
        check_vma=False,
    )
```

profile of v0, /device:TPU:0, one launch (start us, length us, event | category | flops | bytes accessed | tf_op | source)
XLA Modules:
  0.0 1160.1 jit_solution(9391864358575194546)
XLA Ops:
  7.2 10.0 copy.15
  17.2 4.0 broadcast_select_fusion.2
  21.3 5.6 copy-done.2
  26.9 3.0 collective-permute-start
  30.5 3.2 fusion.22
  33.7 11.9 %all-reduce.1 = (f32[512]{0:T(512)S(1)}, f32[512]{0:T(512)S(1)}) all-reduce(f32[512]{0:T(512)S(1)} %get-tuple-element.6, f32[512]{0:T(512)S(1)} %get-tuple-element.5), channel_id=1, replica_groups=mesh['rep'=4,'row'=4,'col'=2] {'row'}, use_global_device_ids=true, to_apply=%region_3.4 | all-reduce | flops 1024 | bytes 8192 | tf_op jit(solution)/shard_map/psum | solution.py:28
  45.7 0.2 convolution_reduce_fusion.1
  45.9 3.6 multiply_convert_fusion.1
  49.6 217.2 %collective-permute-done = bf16[768,6144]{1,0:T(8,128)(2,1)} collective-permute-done((bf16[768,6144]{1,0:T(8,128)(2,1)}, bf16[768,6144]{1,0:T(8,128)(2,1)}, u32[]{:S(2)}, u32[]{:S(2)}) %collective-permute-start) | collective-permute-done | bytes 9437216 | tf_op jit(solution)/shard_map/ppermute | solution.py:16
  266.8 9.7 broadcast_select_fusion.1
  276.5 21.6 %pad_maximum_fusion = bf16[1536,6144]{1,0:T(8,128)(2,1)} fusion(bf16[768,6144]{1,0:T(8,128)(2,1)S(1)} %get-tuple-element.13, bf16[768,6144]{1,0:T(8,128)(2,1)S(1)} %get-tuple-element.12), kind=kLoop, calls=%fused_computation | loop fusion | flops 37748736 | bytes 37748736 | tf_op jit(solution)/shard_map/concatenate | solution.py:89
  298.1 26.1 %fusion.24 = f32[1024,6144]{1,0:T(8,128)} fusion(bf16[1024,1536]{1,0:T(8,128)(2,1)} %all-gather.3.cloned.1.call-done, bf16[1536,6144]{1,0:T(8,128)(2,1)} %pad_maximum_fusion), kind=kOutput, calls=%fused_computation.54 | convolution fusion | flops 19327352832 | bytes 47185920 | tf_op jit(solution)/shard_map/dot_general | solution.py:96
  324.3 1.2 copy-done.3
  325.5 0.5 fusion.15
  326.0 414.1 %reduce-scatter.3.cloned.1.call-done = f32[256,6144]{1,0:T(8,128)} async-done(((f32[1024,6144]{1,0:T(8,128)}), f32[256,6144]{1,0:T(8,128)}) %reduce-scatter.3.cloned.1.call-update) | async-done | bytes 6291472 | tf_op jit(solution)/shard_map/reduce_scatter | solution.py:101
  740.1 15.9 %fusion.2 = bf16[256,6144]{1,0:T(8,128)(2,1)} fusion(f32[256,6144]{1,0:T(8,128)} %reduce-scatter.3.cloned.1.call-done, f32[6144]{0:T(1024)S(1)} %bitcast.36), kind=kLoop, calls=%fused_computation.11 | loop fusion | flops 103809024 | bytes 9461760 | tf_op jit(solution)/shard_map/convert_element_type | solution.py:102
  756.0 0.2 reduce-scatter.5.cloned.1.call-start
  756.3 7.5 fusion.23
  763.8 1.1 bitcast_select_fusion.1
  764.8 1.5 collective-permute-start.1
  766.4 203.3 %collective-permute-done.1 = bf16[6144,768]{1,0:T(8,128)(2,1)} collective-permute-done((bf16[6144,768]{1,0:T(8,128)(2,1)S(1)}, bf16[6144,768]{1,0:T(8,128)(2,1)}, u32[]{:S(2)}, u32[]{:S(2)}) %collective-permute-start.1) | collective-permute-done | bytes 9437216 | tf_op jit(solution)/shard_map/ppermute | solution.py:16
  969.7 9.6 bitcast_select_fusion.2
  979.3 14.5 %pad_maximum_fusion.1 = bf16[6144,1536]{1,0:T(8,128)(2,1)} fusion(bf16[6144,768]{1,0:T(8,128)(2,1)} %get-tuple-element.17, bf16[6144,768]{1,0:T(8,128)(2,1)S(1)} %get-tuple-element.16), kind=kLoop, calls=%fused_computation.1 | loop fusion | flops 37748736 | bytes 37748736 | tf_op jit(solution)/shard_map/concatenate | solution.py:90
  993.8 26.1 %fusion.25 = f32[1024,1536]{1,0:T(8,128)} fusion(bf16[1024,6144]{1,0:T(8,128)(2,1)} %all-gather.5.cloned.1.call-done, bf16[6144,1536]{1,0:T(8,128)(2,1)} %pad_maximum_fusion.1), kind=kOutput, calls=%fused_computation.55 | convolution fusion | flops 19327352832 | bytes 37748736 | tf_op jit(solution)/shard_map/dot_general | solution.py:103
  1020.0 0.9 copy-done.6
  1020.9 0.2 convolution_reduce_fusion
  1021.1 78.1 %reduce-scatter.5.cloned.1.call-done = f32[512,1536]{1,0:T(8,128)} async-done(((f32[1024,1536]{1,0:T(8,128)}), f32[512,1536]{1,0:T(8,128)}) %reduce-scatter.5.cloned.1.call-update) | async-done | bytes 3145744 | tf_op jit(solution)/shard_map/reduce_scatter | solution.py:110
  1099.2 4.8 fusion.21
  1104.0 11.7 %all-reduce = (f32[512]{0:T(512)S(1)}, f32[512]{0:T(512)S(1)}) all-reduce(f32[512]{0:T(512)S(1)} %get-tuple-element.4, f32[512]{0:T(512)S(1)} %get-tuple-element.3), channel_id=1, replica_groups=mesh['rep'=4,'row'=4,'col'=2] {'row'}, use_global_device_ids=true, to_apply=%region_9.10 | all-reduce | flops 1024 | bytes 8192 | tf_op jit(solution)/shard_map/psum | solution.py:28
  1115.7 3.2 fusion.10
  1119.0 33.0 %all-reduce.4.cloned.1.call-done = f32[512,128]{1,0:T(8,128)} async-done(((f32[512,128]{1,0:T(8,128)}), f32[512,128]{1,0:T(8,128)}) %all-reduce.4.cloned.1.call-update) | async-done | bytes 262160 | tf_op jit(solution)/shard_map/psum | solution.py:114
  1151.9 1.7 copy.18
  (30 shorter events, 0.3 us)
Async XLA Ops:
  7.2 23.3 %copy-start = (bf16[588,1536]{1,0:T(8,128)(2,1)S(1)}, bf16[588,1536]{1,0:T(8,128)(2,1)}, u32[]{:S(2)}) copy-start(bf16[588,1536]{1,0:T(8,128)(2,1)} %param.12) | copy-start | bytes 5419012
  7.2 291.0 %all-gather.3.cloned.1.call-start = ((), (), s32[]{:S(2)}) async-start(), calls=%async_computation.2 | async-start | bytes 4718592 | tf_op jit(solution)/shard_map/all_gather | solution.py:97
  17.2 9.7 copy-start.2
  17.2 13.3 %copy-start.8 = (bf16[512,588]{0,1:T(8,128)(2,1)S(1)}, bf16[512,588]{0,1:T(8,128)(2,1)}, u32[]{:S(2)}) copy-start(bf16[512,588]{0,1:T(8,128)(2,1)} %param.11) | copy-start | bytes 1806340
  17.2 13.3 %copy-start.9 = (f32[1536]{0:T(1024)S(1)}, f32[1536]{0:T(1024)}, u32[]{:S(2)}) copy-start(f32[1536]{0:T(1024)} %param.13) | copy-start | bytes 18436
  26.9 18.8 %copy-start.5 = (f32[48,1536]{1,0:T(8,128)S(1)}, f32[48,1536]{1,0:T(8,128)}, u32[]{:S(2)}) copy-start(f32[48,1536]{1,0:T(8,128)} %param.17) | copy-start | bytes 884740
  26.9 239.9 %collective-permute-start = (bf16[768,6144]{1,0:T(8,128)(2,1)}, bf16[768,6144]{1,0:T(8,128)(2,1)}, u32[]{:S(2)}, u32[]{:S(2)}) collective-permute-start(bf16[768,6144]{1,0:T(8,128)(2,1)} %broadcast_select_fusion.2), channel_id=1, source_target_pairs={{0,1},{1,0},{2,3},{3,2},{4,5},{5,4},{6,7},{7,6},{8,9},{9,8},{10,11... | collective-permute-start | bytes 28311560 | tf_op jit(solution)/shard_map/ppermute | solution.py:16
  49.5 690.6 %reduce-scatter.3.cloned.1.call-start = ((), (), s32[]{:S(2)}) async-start(), calls=%async_computation.3 | async-start | bytes 31457280 | tf_op jit(solution)/shard_map/reduce_scatter | solution.py:101
  324.3 1.3 copy-start.3
  324.3 669.5 %all-gather.5.cloned.1.call-start = ((), (), s32[]{:S(2)}) async-start(), calls=%async_computation.4 | async-start | bytes 15728640 | tf_op jit(solution)/shard_map/all_gather | solution.py:104
  756.0 343.1 %reduce-scatter.5.cloned.1.call-start = ((), (), s32[]{:S(2)}) async-start(), calls=%async_computation.5 | async-start | bytes 9437184 | tf_op jit(solution)/shard_map/reduce_scatter | solution.py:110
  764.8 204.9 %collective-permute-start.1 = (bf16[6144,768]{1,0:T(8,128)(2,1)S(1)}, bf16[6144,768]{1,0:T(8,128)(2,1)}, u32[]{:S(2)}, u32[]{:S(2)}) collective-permute-start(bf16[6144,768]{1,0:T(8,128)(2,1)S(1)} %bitcast_select_fusion.1), channel_id=1, source_target_pairs={{0,1},{1,0},{2,3},{3,2},{4,5},{5,4},{6,7},{7,6},{8,9},{9,8},{10,11... | collective-permute-start | bytes 28311560 | tf_op jit(solution)/shard_map/ppermute | solution.py:16
  1019.9 1.0 copy-start.6
  1020.0 95.8 %copy-start.4 = (bf16[1536,128]{1,0:T(8,128)(2,1)S(1)}, bf16[1536,128]{1,0:T(8,128)(2,1)}, u32[]{:S(2)}) copy-start(bf16[1536,128]{1,0:T(8,128)(2,1)} %param.21) | copy-start | bytes 1179652
  1020.0 95.7 %copy-start.7 = (f32[1536]{0:T(1024)S(1)}, f32[1536]{0:T(1024)}, u32[]{:S(2)}) copy-start(f32[1536]{0:T(1024)} %param.20) | copy-start | bytes 18436
  1020.0 132.0 %all-reduce.4.cloned.1.call-start = ((), (), s32[]{:S(2)}) async-start(), calls=%async_computation.6 | async-start | bytes 524288 | tf_op jit(solution)/shard_map/psum | solution.py:114
  1020.9 132.7 %copy-start.1 = (bf16[588,1536]{1,0:T(8,128)(2,1)S(1)}, bf16[588,1536]{1,0:T(8,128)(2,1)}, u32[]{:S(2)}) copy-start(bf16[588,1536]{1,0:T(8,128)(2,1)} %param.12) | copy-start | bytes 5419012
Sparse Core Ops, SparseCore 0:
  49.6 75.9 all-gather.2
  324.4 415.6 reduce-scatter.2
  756.2 220.1 all-gather.4
  1020.1 79.0 reduce-scatter.4
  1119.1 32.8 all-reduce.3
where the time goes:
time: 1160 us
  waiting for transfers between devices  946 us (82%)
  other arithmetic  84.8 us (7%)
  matrix products  59.6 us (5%)
  local copies, waits for them, and re-layouts  26.9 us (2%)
  blocking collectives  23.6 us (2%)
  between operations  14.6 us (1%)
    ppermute x2, waiting for transfers between devices, partner(): return lax.ppermute(value, axis, pairs)  421 us
    reduce_scatter x1, waiting for transfers between devices, on_device(): lax.psum_scatter(partial_pre, 'row', scatter_dimension=0, tiled=True)  414 us
    reduce_scatter x1, waiting for transfers between devices, on_device(): lax.psum_scatter(partial_branch, 'col', scatter_dimension=0, tiled=True)  78.1 us
    psum x1, waiting for transfers between devices, on_device(): lax.psum(jnp.dot(final_normed, check_weight, preferred_element_type=jnp.f...  33 us
    dot_general x1, matrix products, on_device(): jnp.dot(lax.all_gather(hidden, 'row', axis=0, tiled=True), out_weight, pr...  26.1 us
    dot_general x1, matrix products, on_device(): jnp.dot(lax.all_gather(normed, 'col', axis=0, tiled=True), in_weight, pre...  26.1 us
    psum x2, blocking collectives, norm_rows(): lax.psum((jnp.sum(values, axis=1), jnp.sum(values * values, axis=1)), 'row')  23.6 us
  transfers between devices with their start and end apart: 7, of which 5 were waited for; matrix products, arithmetic and copies ran while one was open for 6% of the time, Pallas kernels for 0%

commit v1 on v0

--- a/solution.py
+++ b/solution.py
@@ -4,6 +4,7 @@
 from jax.sharding import PartitionSpec as P
 
 EPSILON = 1e-06
+CHUNKS = 2
 
 
 def for_sending(shard):
@@ -50,6 +51,76 @@
     return pieces
 
 
+def butterfly_weights(old_in, old_out):
+    tiles_here, tile_rows, tile_cols = old_in.shape
+    local_cols = tiles_here * tile_cols
+    half_cols = local_cols // 2
+    in_local = jnp.transpose(old_in, (1, 0, 2)).reshape(tile_rows, local_cols)
+    out_local = old_out.reshape(local_cols, tile_rows)
+    col_index = lax.axis_index("col")
+    col_count = lax.axis_size("col")
+    col_bits = col_count.bit_length() - 1
+    pieces = (
+        (in_local[:, :half_cols], in_local[:, half_cols:]),
+        (out_local[:half_cols], out_local[half_cols:]),
+    )
+    pieces = move_halves(
+        pieces,
+        col_bits,
+        col_index,
+        lambda send_parts, bit_number: jax.tree.map(
+            lambda part, own: part.astype(own.dtype),
+            partner(for_sending(send_parts), "col", bit_number),
+            send_parts,
+        ),
+    )
+    in_pair, out_pair = pieces
+    in_weight = jnp.concatenate(in_pair, axis=0)
+    out_weight = jnp.concatenate(out_pair, axis=1)
+    return in_weight, out_weight
+
+
+def shared_exchange(old_in, old_out):
+    tiles_here, tile_rows, tile_cols = old_in.shape
+    half_tiles = tiles_here // 2
+    half_cols = half_tiles * tile_cols
+    col_index = lax.axis_index("col")
+    rep_index = lax.axis_index("rep")
+    rep_count = lax.axis_size("rep")
+    in_parts = old_in.reshape(2, rep_count, half_tiles * tile_rows // rep_count, tile_cols)
+    share = lax.dynamic_slice(
+        in_parts, (1 - col_index, rep_index, 0, 0), (1, 1) + in_parts.shape[2:]
+    )[0, 0]
+    share = partner(share, "col", 0)
+    out_parts = old_out.reshape(2, half_cols, tile_rows)
+    out_sent = lax.dynamic_index_in_dim(out_parts, 1 - col_index, 0, keepdims=False)
+    out_kept = lax.dynamic_index_in_dim(out_parts, col_index, 0, keepdims=False)
+    share, out_sent = lax.optimization_barrier((share, out_sent))
+    out_arrived = partner(out_sent, "col", 0)
+    in_arrived = lax.all_gather(share, "rep", axis=0, tiled=True)
+
+    def as_rows(tiles):
+        rows = tiles.reshape(half_tiles, tile_rows, tile_cols)
+        return jnp.transpose(rows, (1, 0, 2)).reshape(1, tile_rows, half_cols)
+
+    kept = as_rows(lax.dynamic_index_in_dim(in_parts, col_index, 0, keepdims=False))
+    blocks = jnp.zeros((2, tile_rows, half_cols), old_in.dtype)
+    blocks = lax.dynamic_update_slice(blocks, kept, (col_index, 0, 0))
+    blocks = lax.dynamic_update_slice(blocks, as_rows(in_arrived), (1 - col_index, 0, 0))
+    return blocks.reshape(2 * tile_rows, half_cols), out_kept, out_arrived
+
+
+def join_out(out_kept, out_arrived):
+    upper_side = lax.axis_index("col") == 1
+    return jnp.concatenate(
+        (
+            jnp.where(upper_side, out_arrived, out_kept),
+            jnp.where(upper_side, out_kept, out_arrived),
+        ),
+        axis=1,
+    )
+
+
 def on_device(
     patches,
     embed_weight,
@@ -63,51 +134,53 @@
     final_gain,
     check_weight,
 ):
-    tiles_here, tile_rows, tile_cols = old_in.shape
-    local_cols = tiles_here * tile_cols
-    half_cols = local_cols // 2
-    in_local = jnp.transpose(old_in, (1, 0, 2)).reshape(tile_rows, local_cols)
-    out_local = old_out.reshape(local_cols, tile_rows)
-    col_index = lax.axis_index("col")
-    col_count = lax.axis_size("col")
-    col_bits = col_count.bit_length() - 1
-    pieces = (
-        (in_local[:, :half_cols], in_local[:, half_cols:]),
-        (out_local[:half_cols], out_local[half_cols:]),
-    )
-    pieces = move_halves(
-        pieces,
-        col_bits,
-        col_index,
-        lambda send_parts, bit_number: jax.tree.map(
-            lambda part, own: part.astype(own.dtype),
-            partner(for_sending(send_parts), "col", bit_number),
-            send_parts,
-        ),
-    )
-    in_pair, out_pair = pieces
-    in_weight = jnp.concatenate(in_pair, axis=0)
-    out_weight = jnp.concatenate(out_pair, axis=1)
+    paired = (
+        lax.axis_size("col") == 2
+        and old_in.shape[0] % 2 == 0
+        and (old_in.shape[0] // 2 * old_in.shape[1]) % lax.axis_size("rep") == 0
+    )
+    if paired:
+        in_weight, out_kept, out_arrived = shared_exchange(old_in, old_out)
+    else:
+        in_weight, out_weight = butterfly_weights(old_in, old_out)
     layer_gain = pick_rows(restore_id, norm_gains)
     in_bias = pick_rows(restore_id, in_biases)
     out_bias = pick_rows(restore_id, out_biases)
     embedded = jnp.dot(patches, embed_weight, preferred_element_type=jnp.float32) + embed_bias
     normed = norm_rows(embedded, layer_gain)
-    partial_pre = jnp.dot(
-        lax.all_gather(normed, "col", axis=0, tiled=True),
-        in_weight,
-        preferred_element_type=jnp.float32,
-    )
-    pre_share = lax.psum_scatter(partial_pre, "row", scatter_dimension=0, tiled=True) + in_bias
-    hidden = jax.nn.gelu(pre_share, approximate=False).astype(jnp.bfloat16)
-    partial_branch = jnp.dot(
-        lax.all_gather(hidden, "row", axis=0, tiled=True),
-        out_weight,
-        preferred_element_type=jnp.float32,
+    tokens = lax.all_gather(normed, "col", axis=0, tiled=True)
+    chunk_rows = tokens.shape[0] // CHUNKS
+    pre_shares = []
+    for chunk in range(CHUNKS):
+        partial_pre = jnp.dot(
+            tokens[chunk * chunk_rows : (chunk + 1) * chunk_rows],
+            in_weight,
+            preferred_element_type=jnp.float32,
+        ).astype(jnp.bfloat16)
+        pre_shares.append(
+            lax.psum_scatter(partial_pre, "row", scatter_dimension=0, tiled=True)
+        )
+    hidden_chunks = [
+        jax.nn.gelu(share.astype(jnp.float32) + in_bias, approximate=False).astype(jnp.bfloat16)
+        for share in pre_shares
+    ]
+    if paired:
+        hidden_chunks[0], out_arrived = lax.optimization_barrier((hidden_chunks[0], out_arrived))
+        out_weight = join_out(out_kept, out_arrived)
+    partial_branch = jnp.concatenate(
+        [
+            jnp.dot(
+                lax.all_gather(hidden, "row", axis=0, tiled=True),
+                out_weight,
+                preferred_element_type=jnp.float32,
+            ).astype(jnp.bfloat16)
+            for hidden in hidden_chunks
+        ],
+        axis=0,
     )
     updated = (
         embedded
-        + lax.psum_scatter(partial_branch, "col", scatter_dimension=0, tiled=True)
+        + lax.psum_scatter(partial_branch, "col", scatter_dimension=0, tiled=True).astype(jnp.float32)
         + out_bias
     )
     final_normed = norm_rows(updated, final_gain)

time: 1160 us -> 786 us (0.68)
  waiting for transfers between devices: 946 us -> 532 us
  local copies, waits for them, and re-layouts: 26.9 us -> 97.8 us
  other arithmetic: 84.8 us -> 40.4 us
    ppermute x2, waiting for transfers between devices: 421 us -> 43.6 us  [partner(): return lax.ppermute(value, axis, pairs)]
    reduce_scatter x1 -> x2, waiting for transfers between devices: 414 us -> 206 us  [on_device(): lax.psum_scatter(partial_pre, 'row', scatter_dimension=0, tiled=True)]
    all_gather x1 -> x2, waiting for transfers between devices: 0.01 us -> 199 us  [on_device(): lax.all_gather(hidden, 'row', axis=0, tiled=True)]
    reduce_scatter x1, waiting for transfers between devices: 78.1 us -> 40.6 us  [on_device(): lax.psum_scatter(partial_branch, 'col', scatter_dimension=0, tiled=True)]
    transpose x0 -> x3, local copies, waits for them, and re-layouts: none -> 33.5 us  [as_rows(): return jnp.transpose(rows, (1, 0, 2)).reshape(1, tile_rows, half_cols)]
    concatenate x2, other arithmetic: 36.1 us -> 9.85 us  [the longest x1 8 us: join_out(): jnp.concatenate((jnp.where(upper_side, out_arrived, out_kept), jnp.where(...]
    dynamic_update_slice x0 -> x2, local copies, waits for them, and re-layouts: none -> 17.2 us  [the longest x1 8.6 us: shared_exchange(): blocks = lax.dynamic_update_slice(blocks, kept, (col_index, 0, 0))]
    select_n x4 -> x1, other arithmetic: 24.4 us -> 7.74 us  [join_out(): jnp.where(upper_side, out_arrived, out_kept)]
  transfers between devices with their start and end apart: 7 -> 10, of which waited for: 5 -> 8; matrix products, arithmetic and copies ran while one was open for 6% -> 21% of each run, Pallas kernels for 0% -> 0%
where the time goes in v1:
time: 786 us; the launch traced here: 784 us
  waiting for transfers between devices  532 us (68%)
  local copies, waits for them, and re-layouts  97.8 us (12%)
  matrix products  70.9 us (9%)
  other arithmetic  40.4 us (5%)
  blocking collectives  23.9 us (3%)
  between operations  14.9 us (2%)
    reduce_scatter x2, waiting for transfers between devices, on_device(): lax.psum_scatter(partial_pre, 'row', scatter_dimension=0, tiled=True)  206 us
    all_gather x2, waiting for transfers between devices, on_device(): lax.all_gather(hidden, 'row', axis=0, tiled=True)  199 us
    ppermute x2, waiting for transfers between devices, partner(): return lax.ppermute(value, axis, pairs)  43.6 us
    reduce_scatter x1, waiting for transfers between devices, on_device(): lax.psum_scatter(partial_branch, 'col', scatter_dimension=0, tiled=True)  40.6 us
    transpose x3, local copies, waits for them, and re-layouts, as_rows(): return jnp.transpose(rows, (1, 0, 2)).reshape(1, tile_rows, half_cols)  33.5 us
    psum x1, waiting for transfers between devices, on_device(): lax.psum(jnp.dot(final_normed, check_weight, preferred_element_type=jnp.f...  33 us
    dot_general x2, matrix products, on_device(): jnp.dot(tokens[chunk * chunk_rows:(chunk + 1) * chunk_rows], in_weight, p...  32 us
    dot_general x2, matrix products, on_device(): jnp.dot(lax.all_gather(hidden, 'row', axis=0, tiled=True), out_weight, pr...  31.1 us
  transfers between devices with their start and end apart: 10, of which 8 were waited for; matrix products, arithmetic and copies ran while one was open for 21% of the time, Pallas kernels for 0%

profile of v1, /device:TPU:0, one launch (start us, length us, event | category | flops | bytes accessed | tf_op | source)
XLA Modules:
  0.0 784.1 jit_solution(532455268089544893)
XLA Ops:
  7.2 3.3 dynamic-slice_bitcast_fusion.2
  10.6 3.0 collective-permute-start
  13.6 8.0 %dynamic-slice_bitcast_fusion = bf16[6144,768]{1,0:T(8,128)(2,1)} fusion(bf16[2,6144,768]{2,1,0:T(8,128)(2,1)} %bitcast.50, s32[]{:T(128)S(6)} %select_n.28), kind=kLoop, calls=%fused_computation.3 | loop fusion | bytes 18874372 | tf_op jit(solution)/shard_map/jit(dynamic_index_in_dim)/squeeze | solution.py:96
  21.5 43.6 %collective-permute-done = bf16[768,1536]{1,0:T(8,128)(2,1)} collective-permute-done((bf16[768,1536]{1,0:T(8,128)(2,1)}, bf16[768,1536]{1,0:T(8,128)(2,1)}, u32[]{:S(2)}, u32[]{:S(2)}) %collective-permute-start) | collective-permute-done | bytes 2359328 | tf_op jit(solution)/shard_map/ppermute | solution.py:17
  65.9 3.3 fusion.40
  69.2 12.2 %all-reduce.1 = (f32[512]{0:T(512)S(1)}, f32[512]{0:T(512)S(1)}) all-reduce(f32[512]{0:T(512)S(1)} %get-tuple-element.14, f32[512]{0:T(512)S(1)} %get-tuple-element.13), channel_id=1, replica_groups=mesh['rep'=4,'row'=4,'col'=2] {'row'}, use_global_device_ids=true, to_apply=%region_3.4 | all-reduce | flops 1024 | bytes 8192 | tf_op jit(solution)/shard_map/psum | solution.py:29
  81.6 3.5 multiply_convert_fusion.1
  85.2 8.1 %dynamic-slice_bitcast_fusion.1 = bf16[768,4,1536]{2,0,1:T(8,128)(2,1)} fusion(bf16[2,4,768,1536]{3,2,1,0:T(8,128)(2,1)} %bitcast.54, s32[]{:T(128)S(6)} %select_n.27), kind=kLoop, calls=%fused_computation.4 | loop fusion | bytes 18874372 | tf_op jit(solution)/shard_map/transpose | solution.py:104
  93.4 12.6 %copy.14 = bf16[768,4,1536]{0,2,1:T(8,128)(2,1)} copy(bf16[768,4,1536]{2,0,1:T(8,128)(2,1)} %dynamic-slice_bitcast_fusion.1) | data formatting | bytes 18874368 | tf_op jit(solution)/shard_map/transpose | solution.py:104
  106.0 12.6 %copy.15 = bf16[1,768,6144]{2,1,0:T(8,128)(2,1)} copy(bf16[1,768,6144]{1,2,0:T(8,128)(2,1)} %bitcast.45) | data formatting | bytes 18874368 | tf_op jit(solution)/shard_map/reshape | solution.py:104
  118.6 6.7 broadcast_in_dim.2
  125.3 8.6 %constant_dynamic-update-slice_fusion.1 = bf16[2,768,6144]{2,1,0:T(8,128)(2,1)} fusion(bf16[2,768,6144]{2,1,0:T(8,128)(2,1)} %broadcast_in_dim.2, bf16[1,768,6144]{2,1,0:T(8,128)(2,1)} %copy.15, s32[]{:T(128)S(6)} %select_n.27), kind=kLoop, calls=%fused_computation.77 | loop fusion | bytes 18874372 | tf_op jit(solution)/shard_map/dynamic_update_slice | solution.py:108
  133.9 12.8 %copy.16 = bf16[768,4,1536]{0,2,1:T(8,128)(2,1)} copy(bf16[768,4,1536]{2,0,1:T(8,128)(2,1)} %bitcast.52) | data formatting | bytes 18874368 | tf_op jit(solution)/shard_map/transpose | solution.py:104
  146.7 12.7 %copy.17 = bf16[1,768,6144]{2,1,0:T(8,128)(2,1)} copy(bf16[1,768,6144]{1,2,0:T(8,128)(2,1)} %bitcast.46) | data formatting | bytes 18874368 | tf_op jit(solution)/shard_map/reshape | solution.py:104
  159.4 8.6 %constant_dynamic-update-slice_fusion = bf16[2,768,6144]{2,1,0:T(8,128)(2,1)} fusion(bf16[2,768,6144]{2,1,0:T(8,128)(2,1)} %constant_dynamic-update-slice_fusion.1, bf16[1,768,6144]{2,1,0:T(8,128)(2,1)} %copy.17, s32[]{:T(128)S(6)} %select_n.28), kind=kLoop, calls=%fused_computation.76 | loop fusion | bytes 18874372 | tf_op jit(solution)/shard_map/dynamic_update_slice | solution.py:109
  168.0 9.5 %all-gather.7.cloned.1.call-done = bf16[1024,1536]{1,0:T(8,128)(2,1)} async-done(((bf16[512,1536]{1,0:T(8,128)(2,1)}), bf16[1024,1536]{1,0:T(8,128)(2,1)}) %all-gather.7.cloned.1.call-update) | async-done | bytes 3145744 | tf_op jit(solution)/shard_map/all_gather | solution.py:151
  177.5 15.9 %convolution_convert_fusion = bf16[512,6144]{1,0:T(8,128)(2,1)} fusion(bf16[1536,6144]{1,0:T(8,128)(2,1)} %bitcast.47, bf16[1024,1536]{1,0:T(8,128)(2,1)} %all-gather.7.cloned.1.call-done), kind=kOutput, calls=%fused_computation.5 | convolution fusion | flops 9666822144 | bytes 26738688 | tf_op jit(solution)/shard_map/dot_general | solution.py:155
  193.7 16.0 %convolution_convert_fusion.1 = bf16[512,6144]{1,0:T(8,128)(2,1)} fusion(bf16[1536,6144]{1,0:T(8,128)(2,1)} %bitcast.48, bf16[1024,1536]{1,0:T(8,128)(2,1)} %all-gather.7.cloned.1.call-done), kind=kOutput, calls=%fused_computation.6 | convolution fusion | flops 9666822144 | bytes 26738688 | tf_op jit(solution)/shard_map/dot_general | solution.py:155
  211.9 92.5 %reduce-scatter.6.cloned.1.call-done = bf16[128,6144]{1,0:T(8,128)(2,1)} async-done(((bf16[512,6144]{1,0:T(8,128)(2,1)}), bf16[128,6144]{1,0:T(8,128)(2,1)}) %reduce-scatter.6.cloned.1.call-update) | async-done | bytes 1572880 | tf_op jit(solution)/shard_map/reduce_scatter | solution.py:161
  304.4 113.5 %reduce-scatter.4.cloned.1.call-done = bf16[128,6144]{1,0:T(8,128)(2,1)} async-done(((bf16[512,6144]{1,0:T(8,128)(2,1)}), bf16[128,6144]{1,0:T(8,128)(2,1)}) %reduce-scatter.4.cloned.1.call-update) | async-done | bytes 1572880 | tf_op jit(solution)/shard_map/reduce_scatter | solution.py:161
  417.9 16.0 %fusion.5 = (bf16[128,6144]{1,0:T(8,128)(2,1)}, bf16[128,6144]{1,0:T(8,128)(2,1)}) fusion(bf16[128,6144]{1,0:T(8,128)(2,1)} %reduce-scatter.6.cloned.1.call-done, f32[6144]{0:T(1024)S(1)} %bitcast.55, bf16[128,6144]{1,0:T(8,128)(2,1)} %reduce-scatter.4.cloned.1.call-done), kind=kLoop, calls=%fused_computation.15 | loop fusion | flops 105381888 | bytes 6316032 | tf_op jit(solution)/shard_map/convert_element_type | solution.py:164
  434.8 7.7 bitcast_select_fusion.1
  442.5 8.0 %pad_maximum_fusion = bf16[6144,1536]{1,0:T(8,128)(2,1)} fusion(bf16[6144,768]{1,0:T(8,128)(2,1)S(1)} %get-tuple-element.20, bf16[6144,768]{1,0:T(8,128)(2,1)S(1)} %get-tuple-element.19), kind=kLoop, calls=%fused_computation | loop fusion | flops 37748736 | bytes 37748736 | tf_op jit(solution)/shard_map/concatenate | solution.py:115
  450.5 99.4 %all-gather.11.cloned.1.call-done = bf16[512,6144]{1,0:T(8,128)(2,1)} async-done(((bf16[128,6144]{1,0:T(8,128)(2,1)}), bf16[512,6144]{1,0:T(8,128)(2,1)}) %all-gather.11.cloned.1.call-update) | async-done | bytes 6291472 | tf_op jit(solution)/shard_map/all_gather | solution.py:173
  549.9 15.6 %convolution_convert_fusion.2 = bf16[512,1536]{1,0:T(8,128)(2,1)S(1)} fusion(bf16[512,6144]{1,0:T(8,128)(2,1)} %all-gather.11.cloned.1.call-done, bf16[6144,1536]{1,0:T(8,128)(2,1)} %pad_maximum_fusion), kind=kOutput, calls=%fused_computation.58 | convolution fusion | flops 9664462848 | bytes 26738688 | tf_op jit(solution)/shard_map/dot_general | solution.py:172
  565.5 99.4 %all-gather.9.cloned.1.call-done = bf16[512,6144]{1,0:T(8,128)(2,1)} async-done(((bf16[128,6144]{1,0:T(8,128)(2,1)}), bf16[512,6144]{1,0:T(8,128)(2,1)}) %all-gather.9.cloned.1.call-update) | async-done | bytes 6291472 | tf_op jit(solution)/shard_map/all_gather | solution.py:173
  664.9 15.6 %convolution_convert_fusion.3 = bf16[512,1536]{1,0:T(8,128)(2,1)S(1)} fusion(bf16[512,6144]{1,0:T(8,128)(2,1)} %all-gather.9.cloned.1.call-done, bf16[6144,1536]{1,0:T(8,128)(2,1)} %pad_maximum_fusion), kind=kOutput, calls=%fused_computation.59 | convolution fusion | flops 9664462848 | bytes 26738688 | tf_op jit(solution)/shard_map/dot_general | solution.py:172
  683.5 40.6 %reduce-scatter.8.cloned.1.call-done = bf16[512,1536]{1,0:T(8,128)(2,1)} async-done(((bf16[1024,1536]{1,0:T(8,128)(2,1)}), bf16[512,1536]{1,0:T(8,128)(2,1)}) %reduce-scatter.8.cloned.1.call-update) | async-done | bytes 1572880 | tf_op jit(solution)/shard_map/reduce_scatter | solution.py:183
  724.1 3.2 fusion.32
  727.3 11.7 %all-reduce = (f32[512]{0:T(512)S(1)}, f32[512]{0:T(512)S(1)}) all-reduce(f32[512]{0:T(512)S(1)} %get-tuple-element.12, f32[512]{0:T(512)S(1)} %get-tuple-element.11), channel_id=1, replica_groups=mesh['rep'=4,'row'=4,'col'=2] {'row'}, use_global_device_ids=true, to_apply=%region_10.11 | all-reduce | flops 1024 | bytes 8192 | tf_op jit(solution)/shard_map/psum | solution.py:29
  739.0 3.6 fusion.26
  742.7 33.0 %all-reduce.4.cloned.1.call-done = f32[512,128]{1,0:T(8,128)} async-done(((f32[512,128]{1,0:T(8,128)}), f32[512,128]{1,0:T(8,128)}) %all-reduce.4.cloned.1.call-update) | async-done | bytes 262160 | tf_op jit(solution)/shard_map/psum | solution.py:187
  (44 shorter events, 8.4 us)
Async XLA Ops:
  7.2 58.7 %copy-start = (bf16[588,1536]{1,0:T(8,128)(2,1)S(1)}, bf16[588,1536]{1,0:T(8,128)(2,1)}, u32[]{:S(2)}) copy-start(bf16[588,1536]{1,0:T(8,128)(2,1)} %param.12) | copy-start | bytes 5419012
  7.2 126.7 %all-gather.5.cloned.1.call-start = ((), (), s32[]{:S(2)}) async-start(), calls=%async_computation.3 | async-start | bytes 11796480 | tf_op jit(solution)/shard_map/all_gather | solution.py:100
  10.6 54.5 %collective-permute-start = (bf16[768,1536]{1,0:T(8,128)(2,1)}, bf16[768,1536]{1,0:T(8,128)(2,1)}, u32[]{:S(2)}, u32[]{:S(2)}) collective-permute-start(bf16[768,1536]{1,0:T(8,128)(2,1)} %dynamic-slice_bitcast_fusion.2), channel_id=1, source_target_pairs={{0,1},{1,0},{2,3},{3,2},{4,5},{5,4},{6,7},{7,6},{8,9},{9,8},{10,11... | collective-permute-start | bytes 7077896 | tf_op jit(solution)/shard_map/ppermute | solution.py:17
  13.6 52.3 %copy-start.6 = (bf16[512,588]{0,1:T(8,128)(2,1)S(1)}, bf16[512,588]{0,1:T(8,128)(2,1)}, u32[]{:S(2)}) copy-start(bf16[512,588]{0,1:T(8,128)(2,1)} %param.11) | copy-start | bytes 1806340
  13.6 52.3 %copy-start.7 = (f32[1536]{0:T(1024)S(1)}, f32[1536]{0:T(1024)}, u32[]{:S(2)}) copy-start(f32[1536]{0:T(1024)} %param.13) | copy-start | bytes 18436
  65.1 112.4 %all-gather.7.cloned.1.call-start = ((), (), s32[]{:S(2)}) async-start(), calls=%async_computation.4 | async-start | bytes 4718592 | tf_op jit(solution)/shard_map/all_gather | solution.py:151
  65.9 15.5 %copy-start.4 = (f32[48,1536]{1,0:T(8,128)S(1)}, f32[48,1536]{1,0:T(8,128)}, u32[]{:S(2)}) copy-start(f32[48,1536]{1,0:T(8,128)} %param.17) | copy-start | bytes 884740
  85.2 219.2 %reduce-scatter.6.cloned.1.call-start = ((), (), s32[]{:S(2)}) async-start(), calls=%async_computation.7 | async-start | bytes 7864320 | tf_op jit(solution)/shard_map/reduce_scatter | solution.py:161
  193.5 224.4 %reduce-scatter.4.cloned.1.call-start = ((), (), s32[]{:S(2)}) async-start(), calls=%async_computation.5 | async-start | bytes 7864320 | tf_op jit(solution)/shard_map/reduce_scatter | solution.py:161
  209.7 1.3 copy-start.3
  209.7 340.2 %all-gather.11.cloned.1.call-start = ((), (), s32[]{:S(2)}) async-start(), calls=%async_computation.8 | async-start | bytes 7864320 | tf_op jit(solution)/shard_map/all_gather | solution.py:173
  211.5 222.5 %collective-permute-start.1 = (bf16[6144,768]{1,0:T(8,128)(2,1)}, bf16[6144,768]{1,0:T(8,128)(2,1)}, u32[]{:S(2)}, u32[]{:S(2)}) collective-permute-start(bf16[6144,768]{1,0:T(8,128)(2,1)} %dynamic-slice_bitcast_fusion), channel_id=1, source_target_pairs={{0,1},{1,0},{2,3},{3,2},{4,5},{5,4},{6,7},{7,6},{8,9},{9,8},{10,11... | collective-permute-start | bytes 28311560 | tf_op jit(solution)/shard_map/ppermute | solution.py:17
  433.9 231.0 %all-gather.9.cloned.1.call-start = ((), (), s32[]{:S(2)}) async-start(), calls=%async_computation.6 | async-start | bytes 7864320 | tf_op jit(solution)/shard_map/all_gather | solution.py:173
  434.5 289.6 %reduce-scatter.8.cloned.1.call-start = ((), (), s32[]{:S(2)}) async-start(), calls=%async_computation.9 | async-start | bytes 4718592 | tf_op jit(solution)/shard_map/reduce_scatter | solution.py:183
  682.3 1.0 copy-start.5
  682.3 56.7 %copy-start.8 = (f32[1536]{0:T(1024)S(1)}, f32[1536]{0:T(1024)}, u32[]{:S(2)}) copy-start(f32[1536]{0:T(1024)} %param.20) | copy-start | bytes 18436
  682.3 93.3 %all-reduce.4.cloned.1.call-start = ((), (), s32[]{:S(2)}) async-start(), calls=%async_computation.10 | async-start | bytes 524288 | tf_op jit(solution)/shard_map/psum | solution.py:187
  724.1 14.9 %copy-start.2 = (bf16[512,1536]{1,0:T(8,128)(2,1)S(1)}, bf16[512,1536]{1,0:T(8,128)(2,1)}, u32[]{:S(2)}) copy-start(bf16[512,1536]{1,0:T(8,128)(2,1)} %reduce-scatter.8.cloned.1.call-done) | copy-start | bytes 4718596
  739.0 38.3 %copy-start.1 = (bf16[588,1536]{1,0:T(8,128)(2,1)S(1)}, bf16[588,1536]{1,0:T(8,128)(2,1)}, u32[]{:S(2)}) copy-start(bf16[588,1536]{1,0:T(8,128)(2,1)} %param.12) | copy-start | bytes 5419012
Sparse Core Ops, SparseCore 0:
  65.3 65.7 all-gather.4
  132.6 44.8 all-gather.6
  193.6 110.7 reduce-scatter.5
  306.5 111.2 reduce-scatter.3
  434.1 115.8 all-gather.10
  551.3 113.5 all-gather.8
  682.4 41.6 reduce-scatter.7
  742.8 32.8 all-reduce.3
